TPU v7x, 32 devices: a whole 2x2x4 slice. The times are simulated.
32 devices in a mesh: grp: 2 (over y), sp: 4 (over z), sub: 2 (over x), rep: 2 (over core).
Axes of the slice: x: 2, y: 2, z: 4, core: 2. Of those that a mesh axis runs over, the one named last changes fastest.
Arguments:
- field: float32 [512, 32, 32, 128], P(('grp', 'sp', 'rep'), 'sub'), parts along dimension 0, may hold values from -40 to 40, as said below
- mix_weight: float32 [256, 256], replicated, may hold values from -0.375 to 0.375
- factor_x: float32 [256, 32], replicated, may hold values from -6 to 6
- factor_y: float32 [256, 32], replicated, may hold values from -6 to 6
- factor_z: float32 [256, 32], replicated, may hold values from -6 to 6
- norm_gain: float32 [256], replicated, may hold values from 0.5 to 1.5
- norm_bias: float32 [256], replicated, may hold values from -3 to 3
- w_in: float32 [256, 256], replicated, may hold values from -0.375 to 0.375
- b_in: float32 [256], replicated, may hold values from -3 to 3
- w_out: float32 [256, 256], replicated, may hold values from -0.375 to 0.375
- b_out: float32 [256], replicated, may hold values from -3 to 3
Outputs:
- block_out: float32 [512, 32, 32, 128], P('grp', 'sub', ('sp', 'rep')), parts along dimension 0
There are 2 independent parts, one for each index of `grp`. A program takes and returns all parts, laid end to end along the dimension named above; an argument that names none is the same for every part. Nothing has to cross between parts.
Inputs may be any that keep to these rules, and one draw needn't show every extreme that they name: `field`: real values of order one in each channel, with scales that differ between channels.
All inputs are finite; a program needn't handle non-finite values.
Results may differ from a plain program's by a relative error of at most 0.000078.
Values sent between devices are 32-bit elements; how exact they have to be, the bound alone decides.
A program may use at most 128 MiB of HBM per device.

v0:
```python
import math
import functools

import jax
import jax.numpy as jnp
from jax import lax
from jax.experimental import pallas as pl
from jax.experimental.pallas import tpu as pltpu
from jax.sharding import PartitionSpec as P

GROUPS = 32
HIGH = lax.Precision.HIGH
WIDE = ("sp", "rep")


def trig(length, freq, positions):
    phases = (freq[:, None] * positions[None, :]) % length
    angles = 2.0 * math.pi / length * phases.astype(jnp.float32)
    return jnp.cos(angles), jnp.sin(angles)


def kron_pair(cos_a, sin_a, cos_b, sin_b):
    ca, sa = cos_a.T[:, None, :, None], sin_a.T[:, None, :, None]
    cb, sb = cos_b.T[None, :, None, :], sin_b.T[None, :, None, :]
    return ca * cb - sa * sb, sa * cb + ca * sb


def split(value):
    high = value.astype(jnp.bfloat16)
    low = (value - high.astype(jnp.float32)).astype(jnp.bfloat16)
    return high, low


def dot3(left, right):
    lh, ll = left
    rh, rl = right
    d = functools.partial(jnp.dot, preferred_element_type=jnp.float32)
    return d(lh, rh) + (d(lh, rl) + d(ll, rh))


def sum_kernel(
    sizes, field_ref, modes_ref, table_ref, summed_ref, total_ref, acc1, acc2, held, send_sem, recv_sem
):
    step = pl.program_id(0)
    n_sp, n_sub, n_rep = sizes
    count = n_sp * n_sub * n_rep
    me = (lax.axis_index("sp") * n_sub + lax.axis_index("sub")) * n_rep + lax.axis_index("rep")

    def place(index):
        return {
            "sp": index // (n_sub * n_rep),
            "sub": (index // n_rep) % n_sub,
            "rep": index % n_rep,
        }

    @pl.when(step == 0)
    def _():
        barrier = pltpu.get_barrier_semaphore()

        def greet(k, carry):
            pl.semaphore_signal(
                barrier,
                inc=1,
                device_id=place((me + k) % count),
                device_id_type=pl.DeviceIdType.MESH,
            )
            return carry

        lax.fori_loop(1, count, greet, 0)

    chans, cells, width = field_ref.shape
    rank = modes_ref.shape[2]

    @pl.when(step == 0)
    def _():
        acc1[...] = jnp.zeros_like(acc1)
        acc2[...] = jnp.zeros_like(acc2)

    table = split(table_ref[...])
    chunk = 32 if chans % 32 == 0 else chans

    def body(index, carry):
        rows = pl.ds(pl.multiple_of(index * chunk, chunk), chunk)
        modes = modes_ref[rows].reshape(chunk * cells, rank)
        value = dot3(split(modes), table).reshape(chunk, cells, width) + field_ref[rows]
        summed_ref[rows] = value
        acc1[rows] += value
        acc2[rows] += value * value
        return carry

    lax.fori_loop(0, chans // chunk, body, 0)

    @pl.when(step == pl.num_programs(0) - 1)
    def _():
        def row(acc):
            per = jnp.sum(acc[...], axis=1)
            per = jnp.sum(per.reshape(GROUPS, chans // GROUPS, width), axis=1)
            per = jnp.broadcast_to(jnp.sum(per, axis=1, keepdims=True), (GROUPS, 128))
            lanes = lax.broadcasted_iota(jnp.int32, (GROUPS, 128), 1)
            rows = lax.broadcasted_iota(jnp.int32, (GROUPS, 128), 0)
            return jnp.sum(jnp.where(lanes == rows, per, 0.0), axis=0, keepdims=True)

        tile = lax.broadcasted_iota(jnp.int32, (8, 128), 0)
        held[0] = jnp.where(tile == 0, row(acc1), jnp.where(tile == 1, row(acc2), 0.0))
        pl.semaphore_wait(pltpu.get_barrier_semaphore(), count - 1)

        def copy(k):
            return pltpu.make_async_remote_copy(
                src_ref=held.at[0],
                dst_ref=held.at[k],
                send_sem=send_sem.at[k],
                recv_sem=recv_sem.at[k],
                device_id=place((me + k) % count),
                device_id_type=pl.DeviceIdType.MESH,
            )

        def launch(k, carry):
            copy(k).start()
            return carry

        def finish(k, carry):
            copy(k).wait()
            return carry

        lax.fori_loop(1, count, launch, 0)
        lax.fori_loop(1, count, finish, 0)
        total_ref[...] = jnp.sum(held[...], axis=0)


def mlp_kernel(summed_ref, vec_ref, w_in_ref, w_out_ref, out_ref):
    cells = summed_ref.shape[1]
    w_in = split(w_in_ref[...])
    w_out = split(w_out_ref[...])
    vec = vec_ref[...]
    mean, scale, bias = vec[:, 0:1], vec[:, 1:2], vec[:, 2:3]
    b_in, b_out = vec[:, 3:4], vec[:, 4:5]
    pair = 2 if cells % 2 == 0 else 1
    for start in range(0, cells, pair):
        parts = [summed_ref[:, p, :] for p in range(start, start + pair)]
        value = jnp.concatenate(parts, axis=1) if pair > 1 else parts[0]
        normed = (value - mean) * scale + bias
        hidden = dot3(w_in, split(normed)) + b_in
        inner = math.sqrt(2.0 / math.pi) * (hidden + 0.044715 * (hidden * hidden * hidden))
        hidden = hidden * (0.5 * (1.0 + jnp.tanh(inner)))
        result = value + dot3(w_out, split(hidden)) + b_out
        width = summed_ref.shape[2]
        for k in range(pair):
            out_ref[:, start + k, :] = result[:, k * width : (k + 1) * width]


def general(
    field, mix_weight, factor_x, factor_y, factor_z, norm_gain, norm_bias, w_in, b_in, w_out, b_out
):
    wide_count = lax.axis_size(WIDE)
    narrow_count = lax.axis_size("sub")
    own_chans, x_local, ny, nz = field.shape
    chans = own_chans * wide_count
    nx = x_local * narrow_count
    kx, ky, kz = factor_x.shape[1], factor_y.shape[1], factor_z.shape[1]
    y_local = ny // wide_count
    half = kz // 2
    kept = half + 1
    me_sub = lax.axis_index("sub")
    cells = x_local * y_local

    spatial = field.reshape(own_chans, x_local, wide_count, y_local, nz)
    spatial = spatial.transpose(2, 0, 1, 3, 4).reshape(wide_count, own_chans, cells, nz)
    spatial = lax.all_to_all(spatial, WIDE, split_axis=0, concat_axis=0, tiled=True)

    cos_z, sin_z = trig(nz, jnp.arange(kept), jnp.arange(nz))
    forward = jnp.concatenate([cos_z, -sin_z]) / nz
    planes = jnp.einsum("rz,cxyz->rcxy", forward, field, precision=HIGH)
    planes = planes.reshape(2 * kept * own_chans, x_local * ny)

    def freqs(length, count):
        index = jnp.arange(count)
        return jnp.where(index < count // 2, index, length - count + index)

    cos_y, sin_y = trig(ny, freqs(ny, ky), jnp.arange(ny))

    def forward_xy(values, owner):
        cos_x, sin_x = trig(nx, freqs(nx, kx), owner * x_local + jnp.arange(x_local))
        c, s = kron_pair(cos_x, sin_x, cos_y, sin_y)
        c = (c / (nx * ny)).reshape(x_local * ny, kx * ky)
        s = (s / (nx * ny)).reshape(x_local * ny, kx * ky)
        a = jnp.dot(values, jnp.concatenate([c, s], axis=1), precision=HIGH)
        a = a.reshape(2, kept * own_chans, 2, kx * ky)
        return a[0, :, 0] + a[1, :, 1], a[1, :, 0] - a[0, :, 1]

    held = planes
    real, imag = forward_xy(held, me_sub)
    for hop in range(1, narrow_count):
        held = lax.ppermute(held, "sub", [(i, (i + 1) % narrow_count) for i in range(narrow_count)])
        owner = (me_sub - hop + narrow_count) % narrow_count
        more_real, more_imag = forward_xy(held, owner)
        real, imag = real + more_real, imag + more_imag

    start = lax.axis_index(WIDE) * own_chans
    fx = lax.dynamic_slice_in_dim(factor_x, start, own_chans, 0)
    fy = lax.dynamic_slice_in_dim(factor_y, start, own_chans, 0)
    fz = lax.dynamic_slice_in_dim(factor_z, start, own_chans, 0)
    mirror_x = (-jnp.arange(kx)) % kx
    mirror_y = (-jnp.arange(ky)) % ky
    plane_a = (fx[:, :, None] * fy[:, None, :]).reshape(own_chans, kx * ky)
    plane_b = (fx[:, mirror_x][:, :, None] * fy[:, mirror_y][:, None, :]).reshape(own_chans, kx * ky)
    zero = jnp.zeros((own_chans, 1), jnp.float32)
    z_plus = jnp.concatenate([fz[:, :half], zero], axis=1).T
    z_minus = jnp.concatenate([zero, fz[:, half:][:, ::-1]], axis=1).T
    weight = z_plus[:, :, None] * plane_a[None] + z_minus[:, :, None] * plane_b[None]
    weight = weight.reshape(kept * own_chans, kx * ky)
    real, imag = real * weight, imag * weight

    cos_x, sin_x = trig(nx, freqs(nx, kx), me_sub * x_local + jnp.arange(x_local))
    c, s = kron_pair(cos_x, sin_x, cos_y, sin_y)

    def columns(t):
        t = t.reshape(x_local, wide_count, y_local, kx * ky)
        return t.transpose(3, 1, 0, 2).reshape(kx * ky, wide_count * cells)

    c, s = columns(c), columns(s)
    table_re = jnp.concatenate([c, -s])
    table_im = jnp.concatenate([s, c])
    both = jnp.concatenate([real, imag], axis=1)
    back = jnp.stack(
        [jnp.dot(both, table_re, precision=HIGH), jnp.dot(both, table_im, precision=HIGH)]
    )
    back = back.reshape(2 * kept, own_chans, wide_count, cells)
    back = back.transpose(2, 1, 0, 3).reshape(wide_count * own_chans, 2 * kept * cells)
    back, spatial = lax.optimization_barrier((back, spatial))
    back = lax.all_to_all(back, WIDE, split_axis=0, concat_axis=0, tiled=True)
    back = back.reshape(chans, 2 * kept, cells)
    mixed = jnp.einsum("oi,irp->opr", mix_weight, back, precision=HIGH)

    inverse_z = jnp.concatenate([cos_z, -sin_z])
    spatial = spatial.reshape(chans, cells, nz)
    block = 8 if cells % 8 == 0 else cells
    steps = cells // block
    cube = pl.BlockSpec((chans, block, nz), lambda i: (0, i, 0))
    whole = lambda *shape: pl.BlockSpec(shape, lambda i: (0,) * len(shape))
    sizes = (lax.axis_size("sp"), narrow_count, lax.axis_size("rep"))
    count = sizes[0] * sizes[1] * sizes[2]
    summed, stats = pl.pallas_call(
        functools.partial(sum_kernel, sizes),
        grid=(steps,),
        out_shape=(
            jax.ShapeDtypeStruct(spatial.shape, jnp.float32),
            jax.ShapeDtypeStruct((8, 128), jnp.float32),
        ),
        in_specs=[
            cube,
            pl.BlockSpec((chans, block, 2 * kept), lambda i: (0, i, 0)),
            whole(2 * kept, nz),
        ],
        out_specs=(cube, whole(8, 128)),
        scratch_shapes=[pltpu.VMEM((chans, block, nz), jnp.float32)] * 2
        + [
            pltpu.VMEM((count, 8, 128), jnp.float32),
            pltpu.SemaphoreType.DMA((count,)),
            pltpu.SemaphoreType.DMA((count,)),
        ],
        compiler_params=pltpu.CompilerParams(collective_id=0, has_side_effects=True),
        name="sum_stats",
    )(spatial, mixed, inverse_z)

    size = chans // GROUPS
    stats = stats[:2, :GROUPS]
    cells_group = size * nx * ny * nz
    group_mean = stats[0] / cells_group
    group_var = stats[1] / cells_group - group_mean * group_mean
    scale = jnp.repeat(lax.rsqrt(group_var + 1e-05), size) * norm_gain
    mean = jnp.repeat(group_mean, size)
    vec = jnp.stack([mean, scale, norm_bias, b_in, b_out] + [b_out] * 3, axis=1)

    result = pl.pallas_call(
        mlp_kernel,
        grid=(steps,),
        out_shape=jax.ShapeDtypeStruct(spatial.shape, jnp.float32),
        in_specs=[cube, whole(chans, 8), whole(*w_in.shape), whole(*w_out.shape)],
        out_specs=cube,
        name="mlp",
    )(summed, vec, w_in, w_out)
    return result.reshape(chans, x_local, y_local, nz)


MESH = pl.DeviceIdType.MESH
LANES = 128


def cosine(index, length):
    fold = jnp.abs(index.astype(jnp.float32) * (2.0 / length) - 1.0)
    near = jnp.minimum(fold, 1.0 - fold) * math.pi
    square = near * near
    total = jnp.full_like(square, 1.0 / math.factorial(14))
    for power in range(6, -1, -1):
        term = 1.0 / math.factorial(2 * power)
        total = term - square * total
    return jnp.where(fold > 0.5, total, -total)


def log2(value):
    return value.bit_length() - 1


def split3(value):
    high = value.astype(jnp.bfloat16)
    rest = value - high.astype(jnp.float32)
    mid = rest.astype(jnp.bfloat16)
    low = (rest - mid.astype(jnp.float32)).astype(jnp.bfloat16)
    return high, mid, low


def pick(left, right):
    d = functools.partial(jnp.dot, preferred_element_type=jnp.float32)
    a, b, c = split3(right)
    return d(left, a) + (d(left, b) + d(left, c))


def pick_right(left, right):
    d = functools.partial(jnp.dot, preferred_element_type=jnp.float32)
    a, b, c = split3(left)
    return d(a, right) + (d(b, right) + d(c, right))


def iota(shape, axis):
    return lax.broadcasted_iota(jnp.int32, shape, axis)


def fused_kernel(
    dims,
    field_ref, mix_ref, w_in_ref, w_out_ref, fx_ref, fy_ref, fz_ref, gain_ref, bias_ref, b_in_ref, b_out_ref,
    out_ref,
    fld, mats, facs, vecs, g_hi, g_lo, gi_hi, gi_lo, yf_hi, yf_lo, yi_hi, yi_lo, xt_hi, xt_lo, fxs, uv, fy_t, fz_t,
    se, sh, lf, re, rh, pin, mid, bs, lb, ls, rb, rl, held, cols, obuf,
    fld_sem, par_sem, own_sem, e_send, e_recv, h_send, h_recv, x_send, x_recv, b_send, b_recv, l_send, l_recv,
    t_send, t_recv, o_sem,
):
    n_sp, n_sub, n_rep, n_freq = dims
    wide = n_sp * n_rep
    count = wide * n_sub
    own, xy_rows, nz = field_ref.shape
    chans = own * wide
    parts, x_local, _, _ = se.shape[1:]
    y_local = LANES // (nz // (2 * parts))
    width = LANES // y_local
    nx = pin.shape[1]
    ny = xy_rows // x_local
    kz = n_freq
    half = kz // 2
    chain = own // n_sub
    sub8 = chain // 8
    tiles = wide + 1
    ltile = half * ny // LANES
    per_tile = LANES // ny
    lane_y, lane_n = log2(y_local), log2(ny)

    me_sub = lax.axis_index("sub")
    me_wide = lax.axis_index("sp") * n_rep + lax.axis_index("rep")
    me = me_wide * n_sub + me_sub

    def place(w, s):
        return {"sp": w // n_rep, "sub": s, "rep": w % n_rep}

    def place_flat(index):
        return place(index // n_sub, index % n_sub)

    def loop(n, body):
        def step(i, carry):
            body(i)
            return carry

        lax.fori_loop(0, n, step, 0)

    barrier = pltpu.get_barrier_semaphore()

    def greet(k, carry):
        pl.semaphore_signal(barrier, inc=1, device_id=place_flat((me + k) % count), device_id_type=MESH)
        return carry

    lax.fori_loop(1, count, greet, 0)

    xchunks = fld_sem.shape[0]
    xc_size = x_local // xchunks

    def fetch(i):
        rows = pl.ds(i * (xc_size * ny), xc_size * ny)
        return pltpu.make_async_copy(field_ref.at[:, rows], fld.at[:, rows], fld_sem.at[i])

    for i in range(xchunks):
        fetch(i).start()
    params = [(mix_ref, mats.at[0]), (w_in_ref, mats.at[1]), (w_out_ref, mats.at[2])]
    params += [(fx_ref, facs.at[0]), (fy_ref, facs.at[1]), (fz_ref, facs.at[2])]
    params += [(gain_ref, vecs.at[0]), (bias_ref, vecs.at[1]), (b_in_ref, vecs.at[2]), (b_out_ref, vecs.at[3])]
    param_copies = [pltpu.make_async_copy(a, b, par_sem.at[i]) for i, (a, b) in enumerate(params)]
    for copy in param_copies:
        copy.start()

    def coef(j):
        low_k = jnp.where(j == 1, half, j >> 1)
        low_s = jnp.where(j == 1, 0, j & 1)
        high_k = (j + 1) >> 1
        high_s = 1 - (j & 1)
        return jnp.where(j < kz, low_k, high_k), jnp.where(j < kz, low_s, high_s)

    def basis(j, z):
        k, s = coef(j)
        value = cosine((k * z + s * (3 * nz // 4)) & (nz - 1), nz)
        edge = (k == 0) | (k == nz // 2)
        return value * jnp.where(edge, math.sqrt(1.0 / nz), math.sqrt(2.0 / nz))

    def g_entry(rows, columns):
        y_in, z = rows >> log2(nz), rows & (nz - 1)
        j, y_out = columns >> lane_y, columns & (y_local - 1)
        return jnp.where(y_in == y_out, basis(j, z), 0.0)

    size = nz * y_local
    stepr = LANES

    def build_g(i):
        rows = pl.ds(pl.multiple_of(i * stepr, stepr), stepr)
        a = iota((stepr, size), 0) + i * stepr
        b = iota((stepr, size), 1)
        g_hi[rows], g_lo[rows] = split(g_entry(a, b))
        gi_hi[rows], gi_lo[rows] = split(g_entry(b, a))

    loop(size // stepr, build_g)

    lane = iota((1, LANES), 1)

    def e_copy(xc, k):
        w = (me_wide + k) % wide
        xs = pl.ds(xc * xc_size, xc_size)
        return pltpu.make_async_remote_copy(
            src_ref=se.at[w, :, xs],
            dst_ref=re.at[:, xs, pl.ds(pl.multiple_of(me_wide * own, own), own)],
            send_sem=e_send.at[xc, k],
            recv_sem=e_recv.at[xc, k],
            device_id=place(w, me_sub),
            device_id_type=MESH,
        )

    hchunks = h_send.shape[0]
    hc_size = x_local // hchunks

    def h_copy(hc, k):
        w = (me_wide + k) % wide
        xs = pl.ds(hc * hc_size, hc_size)
        return pltpu.make_async_remote_copy(
            src_ref=sh.at[w, xs],
            dst_ref=rh.at[xs, :, pl.ds(pl.multiple_of(me_wide * own, own), own)],
            send_sem=h_send.at[hc, k],
            recv_sem=h_recv.at[hc, k],
            device_id=place(w, me_sub),
            device_id_type=MESH,
        )

    def peers(make, what, n=wide):
        def step(k, carry):
            getattr(make(k), what)()
            return carry

        lax.fori_loop(1, n, step, 0)

    zero = jnp.zeros((own, LANES), jnp.float32)

    def transform(xc, squares):
        fetch(xc).wait()

        def one(d, carry):
            left, sq = carry
            groups = []
            for xi in range(xc_size):
                row = (xc * xc_size + xi) * ny + d * y_local
                groups.append(jnp.concatenate([fld[:, row + y, :] for y in range(y_local)], axis=1))
            value = jnp.concatenate(groups, axis=0)
            res = dot3(split(value), (g_hi[...], g_lo[...]))
            cube = res.reshape(xc_size, own, size)
            xs = pl.ds(xc * xc_size, xc_size)
            for g in range(parts):
                se[d, g, xs] = cube[:, :, g * LANES : (g + 1) * LANES]
                part = cube[:, :, (parts + g) * LANES : (parts + g + 1) * LANES]
                sh[d, xs, g] = part
                sq = sq + jnp.sum(part * part, axis=0)
            more = pltpu.roll(res[:, LANES : 2 * LANES], d * y_local, axis=1)
            left = jnp.where((lane >> lane_y) == d, more, left)
            return left, sq

        left = jnp.zeros((xc_size * own, LANES), jnp.float32)
        left, squares = lax.fori_loop(0, wide, one, (left, squares))
        lf[pl.ds(xc * xc_size, xc_size)] = left.reshape(xc_size, own, LANES)

        @pl.when(xc == 1)
        def _():
            pl.semaphore_wait(barrier, count - 1)

        @pl.when(xc >= 1)
        def _():
            peers(lambda k: e_copy(xc - 1, k), "start")

        return squares

    squares = lax.fori_loop(0, xchunks, transform, zero)
    for copy in param_copies:
        copy.wait()

    def x_src(t, s):
        cs = pl.ds(pl.multiple_of(s * chain, 8), chain)
        return se.at[t, 0, :, cs] if t < wide else lf.at[:, cs]

    def x_dst(t):
        return pin.at[t, pl.ds(me_sub * x_local, x_local)]

    x_copies = []
    for t in range(tiles):
        for k in range(1, n_sub):
            s = (me_sub + k) % n_sub
            x_copies.append(
                pltpu.make_async_remote_copy(
                    src_ref=x_src(t, s),
                    dst_ref=x_dst(t),
                    send_sem=x_send.at[t, k],
                    recv_sem=x_recv.at[t, k],
                    device_id=place(me_wide, s),
                    device_id_type=MESH,
                )
            )
    own_chan = pl.ds(pl.multiple_of(me_wide * own, own), own)
    own_copies = [pltpu.make_async_copy(x_src(t, me_sub), x_dst(t), own_sem.at[t]) for t in range(tiles)]
    own_copies.append(pltpu.make_async_copy(se.at[me_wide], re.at[:, :, own_chan], own_sem.at[tiles]))
    own_copies.append(pltpu.make_async_copy(sh.at[me_wide], rh.at[:, :, own_chan], own_sem.at[tiles + 1]))

    def p_meta(t, r):
        jj = r >> lane_y
        k = jnp.where(jj == 1, half, jj >> 1)
        s = jnp.where(jj == 1, 0, jj & 1)
        y = t * y_local + (r & (y_local - 1))
        rest = t == wide
        k = jnp.where(rest, jnp.where(r < ny, half, -1), k)
        return k, jnp.where(rest, 1, s), jnp.where(rest, r, y)

    def m_meta(t, c):
        part = jnp.where(t >= ltile, 1, 0)
        k = (t - part * ltile) * per_tile + (c >> lane_n)
        rest = t == 2 * ltile
        seat = c & (LANES // 2 - 1)
        k = jnp.where(rest, jnp.where(seat < ny, half, -2), k)
        part = jnp.where(rest, c >> log2(LANES // 2), part)
        return k, part, c & (ny - 1)

    def y_entry(pt, mt, p, m, power):
        kp, s, y = p_meta(pt, p)
        km, part, b = m_meta(mt, m)
        value = cosine((y * b + (ny // 4) * (s + part)) & (ny - 1), ny)
        norm = jnp.where(km == 0, math.sqrt(1.0 / nz), math.sqrt(2.0 / nz))
        scale = norm if power else 1.0 / norm
        if not power:
            scale = scale * (1.0 / nz)
        else:
            scale = 1.0 / scale
        return jnp.where(kp == km, value * scale, 0.0)

    square = (LANES, LANES)
    mtiles = 2 * ltile + 1

    def build_y(i):
        rows = pl.ds(pl.multiple_of(i * LANES, LANES), LANES)
        for t in range(mtiles):
            cut = slice(t * LANES, (t + 1) * LANES)
            a, b = iota(square, 0), iota(square, 1)
            yf_hi[rows, cut], yf_lo[rows, cut] = split(y_entry(i, t, a, b, False))
            yi_hi[rows, cut], yi_lo[rows, cut] = split(y_entry(t, i, b, a, True))

    def build_x(i):
        shape = (LANES, nx * 8)
        row = iota(shape, 0) + i * LANES
        col = iota(shape, 1)
        part = row >> log2(nx * 8)
        a = (row >> 3) & (nx - 1)
        value = cosine(((a * (col >> 3)) + part * (3 * nx // 4)) & (nx - 1), nx)
        value = jnp.where((row & 7) == (col & 7), value, 0.0)
        rows = pl.ds(pl.multiple_of(i * LANES, LANES), LANES)
        xt_hi[rows], xt_lo[rows] = split(value)

    peers(lambda k: e_copy(xchunks - 1, k), "start")
    for copy in x_copies:
        copy.start()
    for copy in own_copies:
        copy.start()
    loop(tiles, build_y)
    loop(2 * nx * 8 // LANES, build_x)

    fy_t[...] = jnp.transpose(facs[1])
    fz_t[...] = jnp.transpose(facs[2])
    first = me_wide * own + me_sub * chain
    bf = jnp.bfloat16
    one_hot = lambda mask: jnp.where(mask, 1.0, 0.0).astype(bf)
    for h in range(sub8):
        base = pl.multiple_of(first + 8 * h, 8)
        a = iota((nx * 8, nx), 0) >> 3
        b = iota((nx * 8, nx), 1)
        mask = iota((nx * 8, chans), 1) == first + 8 * h + (iota((nx * 8, chans), 0) & 7)
        for sign in range(2):
            want = a if sign == 0 else (nx - a) & (nx - 1)
            spread = pick(one_hot(b == want), facs[0])
            column = jnp.sum(jnp.where(mask, spread, 0.0), axis=1, keepdims=True)
            fxs[h, sign] = jnp.broadcast_to(column * (1.0 / (nx * ny)), (nx * 8, LANES))
        fz8, fy8 = fz_t[pl.ds(base, 8), :], fy_t[pl.ds(base, 8), :]
        for t in range(ltile + 1):
            i = iota((kz, LANES), 0)
            seat = iota((kz, LANES), 1)
            k = t * per_tile + (seat >> lane_n) if t < ltile else half
            bb = seat & (ny - 1)
            plus = one_hot(i == (k if t < ltile else -1))
            minus = one_hot((i == kz - k) & (k > 0)) if t < ltile else one_hot(i == half)
            yp, ym = one_hot(i == bb), one_hot(i == ((ny - bb) & (ny - 1)))
            uv[h, 0, t] = pick_right(fz8, plus) * pick_right(fy8, yp)
            uv[h, 1, t] = pick_right(fz8, minus) * pick_right(fy8, ym)

    for copy in own_copies:
        copy.wait()
    for copy in x_copies:
        copy.wait()

    rows8 = nx * 8

    def forward_y(h):
        cs = pl.ds(pl.multiple_of(h * 8, 8), 8)
        value = jnp.concatenate([pin[t, :, cs, :].reshape(rows8, LANES) for t in range(tiles)], axis=1)
        res = dot3(split(value), (yf_hi[...], yf_lo[...]))
        for t in range(mtiles):
            mid[h, t] = res[:, t * LANES : (t + 1) * LANES]

    loop(sub8, forward_y)

    def weights(h, t):
        u = jnp.broadcast_to(uv[h, 0, t][None], (nx, 8, LANES)).reshape(rows8, LANES)
        v = jnp.broadcast_to(uv[h, 1, t][None], (nx, 8, LANES)).reshape(rows8, LANES)
        return fxs[h, 0] * u + fxs[h, 1] * v

    def along_x(value):
        return dot3((xt_hi[...], xt_lo[...]), split(value))

    def pair_x(i):
        h, t = i // ltile, i % ltile
        res = along_x(jnp.concatenate([mid[h, t], mid[h, ltile + t]], axis=1))
        c_re, c_im = res[:rows8, :LANES], res[:rows8, LANES:]
        s_re, s_im = res[rows8:, :LANES], res[rows8:, LANES:]
        w = weights(h, t)
        res = along_x(jnp.concatenate([(c_re + s_im) * w, (c_im - s_re) * w], axis=1))
        c_re, c_im = res[:rows8, :LANES], res[:rows8, LANES:]
        s_re, s_im = res[rows8:, :LANES], res[rows8:, LANES:]
        mid[h, t] = c_re - s_im
        mid[h, ltile + t] = c_im + s_re

    loop(sub8 * ltile, pair_x)

    def rest_x(h):
        sign = jnp.where(lane < LANES // 2, 1.0, -1.0)
        res = along_x(mid[h, 2 * ltile])
        modes = res[:rows8] + sign * pltpu.roll(res[rows8:], LANES // 2, axis=1)
        res = along_x(modes * weights(h, ltile))
        mid[h, 2 * ltile] = res[:rows8] - sign * pltpu.roll(res[rows8:], LANES // 2, axis=1)

    loop(sub8, rest_x)

    def back_y(h):
        cs = pl.ds(pl.multiple_of(h * 8, 8), 8)
        value = jnp.concatenate([mid[h, t] for t in range(mtiles)], axis=1)
        res = dot3(split(value), (yi_hi[...], yi_lo[...]))
        for t in range(tiles):
            cut = res[:, t * LANES : (t + 1) * LANES].reshape(nx, 8, LANES)
            if t < wide:
                bs[t, :, cs, :] = cut
            else:
                lb[:, cs, :] = cut

    loop(sub8, back_y)

    def gather_rest(s):
        def one(x, carry):
            value = lb[s * x_local + x]
            new = []
            for d in range(wide):
                moved = pltpu.roll(value, ((x - d) * y_local + LANES) & (LANES - 1), axis=1)
                new.append(jnp.where((lane >> lane_y) == x, moved, carry[d]))
            return tuple(new)

        start = tuple(jnp.zeros((chain, LANES), jnp.float32) for _ in range(wide))
        done = lax.fori_loop(0, x_local, one, start)
        for d in range(wide):
            ls[s, d] = done[d]

    loop(n_sub, gather_rest)

    b_rows = pl.ds(pl.multiple_of(first, 8), chain)

    def b_copy(k):
        index = (me + k) % count
        w, s = index // n_sub, index % n_sub
        return pltpu.make_async_remote_copy(
            src_ref=bs.at[w, pl.ds(s * x_local, x_local)],
            dst_ref=rb.at[:, b_rows],
            send_sem=b_send.at[k],
            recv_sem=b_recv.at[k],
            device_id=place(w, s),
            device_id_type=MESH,
        )

    def l_copy(k):
        index = (me + k) % count
        w, s = index // n_sub, index % n_sub
        return pltpu.make_async_remote_copy(
            src_ref=ls.at[s, w],
            dst_ref=rl.at[b_rows],
            send_sem=l_send.at[k],
            recv_sem=l_recv.at[k],
            device_id=place(w, s),
            device_id_type=MESH,
        )

    peers(b_copy, "start", count)
    own_b = pltpu.make_async_copy(bs.at[me_wide, pl.ds(me_sub * x_local, x_local)], rb.at[:, b_rows], b_send.at[0])
    own_l = pltpu.make_async_copy(ls.at[me_sub, me_wide], rl.at[b_rows], l_send.at[0])
    own_b.start()
    own_l.start()
    peers(l_copy, "start", count)
    loop(hchunks, lambda hc: peers(lambda k: h_copy(hc, k), "start"))

    eye = iota((chans, chans), 0) == iota((chans, chans), 1)
    for i in range(4):
        column = jnp.sum(jnp.where(eye, vecs[i], 0.0), axis=1, keepdims=True)
        cols[i] = jnp.broadcast_to(column, (chans, LANES))

    own_b.wait()
    own_l.wait()
    peers(b_copy, "wait", count)
    peers(l_copy, "wait", count)
    loop(xchunks, lambda xc: peers(lambda k: e_copy(xc, k), "wait"))
    mix = split(mats[0])
    rest = dot3(mix, split(rl[...]))
    lows = lane < y_local
    blank = jnp.zeros((chans, LANES), jnp.float32)

    def low(i, carry):
        one, two = carry
        spectral = dot3(mix, split(jnp.concatenate([rb[2 * i], rb[2 * i + 1]], axis=1)))
        for j in range(2):
            x = 2 * i + j
            value = re[0, x] + spectral[:, j * LANES : (j + 1) * LANES]
            re[0, x] = value
            one = one + jnp.where(lows, value, 0.0)
            two = two + value * value
            moved = pltpu.roll(rest, (LANES - x * y_local) & (LANES - 1), axis=1)
            value = re[1, x] + jnp.where(lows, moved, 0.0)
            re[1, x] = value
            two = two + value * value
        return one, two

    one, two = lax.fori_loop(0, x_local // 2, low, (blank, blank))

    per_group = chans // GROUPS

    def row(acc, base):
        groups = acc.shape[0] // per_group
        per = jnp.sum(acc.reshape(groups, per_group, LANES), axis=1)
        per = jnp.broadcast_to(jnp.sum(per, axis=1, keepdims=True), (groups, LANES))
        seat = iota((groups, LANES), 1) == iota((groups, LANES), 0) + base
        return jnp.sum(jnp.where(seat, per, 0.0), axis=0, keepdims=True)

    tile = iota((8, LANES), 0)
    sum_one = row(one, 0) * math.sqrt(nz)
    sum_two = row(two, 0) + row(squares, me_wide * (own // per_group))
    held[0] = jnp.where(tile == 0, sum_one, jnp.where(tile == 1, sum_two, 0.0))

    def t_copy(k):
        return pltpu.make_async_remote_copy(
            src_ref=held.at[0],
            dst_ref=held.at[k],
            send_sem=t_send.at[k],
            recv_sem=t_recv.at[k],
            device_id=place_flat((me + k) % count),
            device_id_type=MESH,
        )

    peers(t_copy, "start", count)
    peers(t_copy, "wait", count)
    total = jnp.sum(held[...], axis=0)
    cells_group = per_group * nx * ny * nz
    group_mean = total[0:1] / cells_group
    group_var = total[1:2] / cells_group - group_mean * group_mean
    group_scale = lax.rsqrt(group_var + 1e-05)
    seat = iota((chans, LANES), 1) == iota((chans, LANES), 0) // per_group

    def column_of(value):
        return jnp.sum(jnp.where(seat, value, 0.0), axis=1, keepdims=True)

    scale = column_of(group_scale) * cols[0, :, 0:1]
    shift = cols[1, :, 0:1] - column_of(group_mean) * scale
    cols[4] = jnp.broadcast_to(scale, (chans, LANES))
    cols[5] = jnp.broadcast_to(shift, (chans, LANES))

    def out_copy(hc, slot):
        rows = pl.ds(pl.multiple_of(hc * (hc_size * y_local), 8), hc_size * y_local)
        return pltpu.make_async_copy(obuf.at[slot], out_ref.at[:, rows], o_sem.at[slot])

    def late(hc, carry):
        slot = hc % 2
        peers(lambda k: h_copy(hc, k), "wait")

        @pl.when(hc >= 2)
        def _():
            out_copy(hc - 2, slot).wait()

        w_in, w_out = split(mats[1]), split(mats[2])
        factor, offset = cols[4, :, 0:1], cols[5, :, 0:1]
        b_in, b_out = cols[2, :, 0:1], cols[3, :, 0:1]
        for j in range(hc_size):
            x = hc * hc_size + j
            value = jnp.concatenate([re[g, x] for g in range(parts)] + [rh[x, g] for g in range(parts)], axis=1)
            value = dot3(split(value), (gi_hi[...], gi_lo[...]))
            normed = value * factor + offset
            hidden = dot3(w_in, split(normed)) + b_in
            inner = math.sqrt(2.0 / math.pi) * (hidden + 0.044715 * (hidden * hidden * hidden))
            hidden = hidden * (0.5 * (1.0 + jnp.tanh(inner)))
            result = value + dot3(w_out, split(hidden)) + b_out
            for y in range(y_local):
                obuf[slot, :, j * y_local + y, :] = result[:, y * nz : (y + 1) * nz]
        out_copy(hc, slot).start()
        return carry

    lax.fori_loop(0, hchunks, late, 0)
    out_copy(hchunks - 2, (hchunks - 2) % 2).wait()
    out_copy(hchunks - 1, (hchunks - 1) % 2).wait()


def fused(
    field, mix_weight, factor_x, factor_y, factor_z, norm_gain, norm_bias, w_in, b_in, w_out, b_out
):
    n_sp, n_sub, n_rep = (lax.axis_size(a) for a in ("sp", "sub", "rep"))
    wide, count = n_sp * n_rep, n_sp * n_rep * n_sub
    own, x_local, ny, nz = field.shape
    chans, nx, y_local = own * wide, x_local * n_sub, ny // wide
    kz = factor_z.shape[1]
    chain = own // n_sub
    sub8 = chain // 8
    tiles = wide + 1
    ltile = kz // 2 * ny // LANES
    mtiles = 2 * ltile + 1
    parts = nz * y_local // LANES // 2
    size = nz * y_local
    xchunks, hchunks = 4, x_local * y_local // 8
    f32, bf = jnp.float32, jnp.bfloat16
    vmem = lambda *shape: pltpu.VMEM(shape, f32)
    table = lambda *shape: pltpu.VMEM(shape, bf)
    dma = lambda *shape: pltpu.SemaphoreType.DMA(shape)
    scratch = [
        vmem(own, x_local * ny, nz), vmem(3, chans, chans), vmem(3, kz, chans), vmem(4, 1, chans),
        table(size, size), table(size, size), table(size, size), table(size, size),
        table(tiles * LANES, mtiles * LANES), table(tiles * LANES, mtiles * LANES),
        table(mtiles * LANES, tiles * LANES), table(mtiles * LANES, tiles * LANES),
        table(2 * nx * 8, nx * 8), table(2 * nx * 8, nx * 8),
        vmem(sub8, 2, nx * 8, LANES), vmem(sub8, 2, ltile + 1, 8, LANES), vmem(chans, kz), vmem(chans, kz),
        vmem(wide, parts, x_local, own, LANES), vmem(wide, x_local, parts, own, LANES), vmem(x_local, own, LANES),
        vmem(parts, x_local, chans, LANES), vmem(x_local, parts, chans, LANES),
        vmem(tiles, nx, chain, LANES), vmem(sub8, mtiles, nx * 8, LANES),
        vmem(wide, nx, chain, LANES), vmem(nx, chain, LANES), vmem(n_sub, wide, chain, LANES),
        vmem(x_local, chans, LANES), vmem(chans, LANES), vmem(count, 8, LANES), vmem(6, chans, LANES),
        vmem(2, chans, 8, nz),
        dma(xchunks), dma(10), dma(tiles + 2), dma(xchunks, wide), dma(xchunks, wide), dma(hchunks, wide),
        dma(hchunks, wide), dma(tiles, n_sub), dma(tiles, n_sub), dma(count), dma(count), dma(count), dma(count),
        dma(count), dma(count), dma(2),
    ]
    any_spec = pl.BlockSpec(memory_space=pl.ANY)
    line = lambda v: v.reshape(1, chans)
    result = pl.pallas_call(
        functools.partial(fused_kernel, (n_sp, n_sub, n_rep, kz)),
        out_shape=jax.ShapeDtypeStruct((chans, x_local * y_local, nz), f32),
        in_specs=[any_spec] * 11,
        out_specs=any_spec,
        scratch_shapes=scratch,
        compiler_params=pltpu.CompilerParams(
            collective_id=0, has_side_effects=True, vmem_limit_bytes=VMEM_LIMIT
        ),
        name="fused",
    )(
        field.reshape(own, x_local * ny, nz), mix_weight, w_in, w_out, factor_x.T, factor_y.T, factor_z.T,
        line(norm_gain), line(norm_bias), line(b_in), line(b_out),
    )
    return result.reshape(chans, x_local, y_local, nz)


VMEM_LIMIT = 64 * 1024 * 1024 - 65536


def fits(field, factor_x, factor_y, factor_z):
    n_sub, wide = lax.axis_size("sub"), lax.axis_size(WIDE)
    own, x_local, ny, nz = field.shape
    nx, kz = x_local * n_sub, factor_z.shape[1]
    power = all(v & (v - 1) == 0 for v in (nx, ny, nz, kz))
    if not power or nz != LANES or factor_x.shape[1] != nx or factor_y.shape[1] != ny or ny % wide:
        return False
    y_local = ny // wide
    return (
        kz * y_local == LANES
        and nz == 4 * kz
        and nx == kz == ny
        and own % (8 * n_sub) == 0
        and own % (own * wide // GROUPS) == 0
        and x_local * y_local <= LANES
        and x_local % 4 == 0
        and 8 % y_local == 0
        and (kz // 2 * ny) % LANES == 0
    )


def local(
    field, mix_weight, factor_x, factor_y, factor_z, norm_gain, norm_bias, w_in, b_in, w_out, b_out
):
    run = fused if fits(field, factor_x, factor_y, factor_z) else general
    return run(
        field, mix_weight, factor_x, factor_y, factor_z, norm_gain, norm_bias, w_in, b_in, w_out, b_out
    )


def solution(mesh):
    placed = (P(("grp", "sp", "rep"), "sub", None, None),) + (P(),) * 10
    return jax.shard_map(
        local,
        mesh=mesh,
        in_specs=placed,
        out_specs=P("grp", "sub", ("sp", "rep"), None),
        check_vma=False,
    )
```

profile of v0, /device:TPU:0, one launch (start us, length us, event | category | flops | bytes accessed | tf_op | source)
XLA Modules:
  0.0 287.9 jit_solution(1715266424519691768)
XLA Ops:
  0.0 277.4 %fused.1 = f32[256,64,128]{2,1,0:T(8,128)} custom-call(f32[32,512,128]{2,1,0:T(8,128)} %bitcast.10, f32[256,256]{1,0:T(8,128)} %mix_ref.1, f32[256,256]{1,0:T(8,128)} %w_in_ref.1, f32[256,256]{1,0:T(8,128)} %w_out_ref.1, f32[32,256]{1,0:T(8,128)} %bitcast.11, f32[32,256]{1,0:T(8,128)} %bitcast.12, f32[32,256]{1,0:T(8,128)} %bitcast.13, f32[1,256]{1,0:T(1,128)} %bitcast.14, ...), custom_call_target="tpu_custom_call" | custom-call | tf_op jit(solution)/shard_map/fused/pallas_call | solution.py:874
  277.4 10.5 %copy.13 = f32[256,16,4,128]{3,2,1,0:T(4,128)} copy(f32[256,16,4,128]{3,2,1,0:T(4,128)} %bitcast.9) | data formatting | bytes 16777216
where the time goes:
time: 288 us
  Pallas kernels  277 us (96%)
  local copies, waits for them, and re-layouts  10.5 us (4%)
    pallas_call x1, Pallas kernels, fused(): pl.pallas_call(functools.partial(fused_kernel, (n_sp, n_sub, n_rep, kz)),...  277 us
    unnamed x1, local copies, waits for them, and re-layouts  10.5 us

commit v1 on v0

--- a/solution.py
+++ b/solution.py
@@ -284,6 +284,7 @@
 
 MESH = pl.DeviceIdType.MESH
 LANES = 128
+AHEAD = 3
 
 
 def cosine(index, length):
@@ -330,9 +331,9 @@
     field_ref, mix_ref, w_in_ref, w_out_ref, fx_ref, fy_ref, fz_ref, gain_ref, bias_ref, b_in_ref, b_out_ref,
     out_ref,
     fld, mats, facs, vecs, g_hi, g_lo, gi_hi, gi_lo, yf_hi, yf_lo, yi_hi, yi_lo, xt_hi, xt_lo, fxs, uv, fy_t, fz_t,
-    se, sh, lf, re, rh, pin, mid, bs, lb, ls, rb, rl, held, cols, obuf,
+    se, sh, lf, re, rh, pin, mid, bs, lb, ls, rb, rl, held, cols,
     fld_sem, par_sem, own_sem, e_send, e_recv, h_send, h_recv, x_send, x_recv, b_send, b_recv, l_send, l_recv,
-    t_send, t_recv, o_sem,
+    t_send, t_recv,
 ):
     n_sp, n_sub, n_rep, n_freq = dims
     wide = n_sp * n_rep
@@ -723,7 +724,7 @@
     own_b.start()
     own_l.start()
     peers(l_copy, "start", count)
-    loop(hchunks, lambda hc: peers(lambda k: h_copy(hc, k), "start"))
+    loop(AHEAD, lambda hc: peers(lambda k: h_copy(hc, k), "start"))
 
     eye = iota((chans, chans), 0) == iota((chans, chans), 1)
     for i in range(4):
@@ -798,17 +799,12 @@
     cols[4] = jnp.broadcast_to(scale, (chans, LANES))
     cols[5] = jnp.broadcast_to(shift, (chans, LANES))
 
-    def out_copy(hc, slot):
-        rows = pl.ds(pl.multiple_of(hc * (hc_size * y_local), 8), hc_size * y_local)
-        return pltpu.make_async_copy(obuf.at[slot], out_ref.at[:, rows], o_sem.at[slot])
-
     def late(hc, carry):
-        slot = hc % 2
         peers(lambda k: h_copy(hc, k), "wait")
 
-        @pl.when(hc >= 2)
+        @pl.when(hc + AHEAD < hchunks)
         def _():
-            out_copy(hc - 2, slot).wait()
+            peers(lambda k: h_copy(hc + AHEAD, k), "start")
 
         w_in, w_out = split(mats[1]), split(mats[2])
         factor, offset = cols[4, :, 0:1], cols[5, :, 0:1]
@@ -823,13 +819,10 @@
             hidden = hidden * (0.5 * (1.0 + jnp.tanh(inner)))
             result = value + dot3(w_out, split(hidden)) + b_out
             for y in range(y_local):
-                obuf[slot, :, j * y_local + y, :] = result[:, y * nz : (y + 1) * nz]
-        out_copy(hc, slot).start()
+                out_ref[:, x * y_local + y, :] = result[:, y * nz : (y + 1) * nz]
         return carry
 
     lax.fori_loop(0, hchunks, late, 0)
-    out_copy(hchunks - 2, (hchunks - 2) % 2).wait()
-    out_copy(hchunks - 1, (hchunks - 1) % 2).wait()
 
 
 def fused(
@@ -864,18 +857,17 @@
         vmem(tiles, nx, chain, LANES), vmem(sub8, mtiles, nx * 8, LANES),
         vmem(wide, nx, chain, LANES), vmem(nx, chain, LANES), vmem(n_sub, wide, chain, LANES),
         vmem(x_local, chans, LANES), vmem(chans, LANES), vmem(count, 8, LANES), vmem(6, chans, LANES),
-        vmem(2, chans, 8, nz),
         dma(xchunks), dma(10), dma(tiles + 2), dma(xchunks, wide), dma(xchunks, wide), dma(hchunks, wide),
         dma(hchunks, wide), dma(tiles, n_sub), dma(tiles, n_sub), dma(count), dma(count), dma(count), dma(count),
-        dma(count), dma(count), dma(2),
+        dma(count), dma(count),
     ]
     any_spec = pl.BlockSpec(memory_space=pl.ANY)
     line = lambda v: v.reshape(1, chans)
     result = pl.pallas_call(
         functools.partial(fused_kernel, (n_sp, n_sub, n_rep, kz)),
-        out_shape=jax.ShapeDtypeStruct((chans, x_local * y_local, nz), f32),
+        out_shape=pltpu.VMEM((chans, x_local * y_local, nz), f32),
         in_specs=[any_spec] * 11,
-        out_specs=any_spec,
+        out_specs=pl.BlockSpec(memory_space=pltpu.VMEM),
         scratch_shapes=scratch,
         compiler_params=pltpu.CompilerParams(
             collective_id=0, has_side_effects=True, vmem_limit_bytes=VMEM_LIMIT
@@ -888,7 +880,7 @@
     return result.reshape(chans, x_local, y_local, nz)
 
 
-VMEM_LIMIT = 64 * 1024 * 1024 - 65536
+VMEM_LIMIT = 55 * 1024 * 1024
 
 
 def fits(field, factor_x, factor_y, factor_z):

time: 288 us -> 256 us (0.89)
  Pallas kernels: 277 us -> 251 us
  local copies, waits for them, and re-layouts: 10.5 us -> 3.4 us
    pallas_call x1, Pallas kernels: 277 us -> 251 us  [fused(): pl.pallas_call(functools.partial(fused_kernel, (n_sp, n_sub, n_rep, kz)),...]
    unnamed x1, local copies, waits for them, and re-layouts: 10.5 us -> 3.4 us
where the time goes in v1:
time: 256 us; the launch traced here: 255 us
  Pallas kernels  251 us (98%)
  local copies, waits for them, and re-layouts  3.4 us (1%)
    pallas_call x1, Pallas kernels, fused(): pl.pallas_call(functools.partial(fused_kernel, (n_sp, n_sub, n_rep, kz)),...  251 us

profile of v1, /device:TPU:0, one launch (start us, length us, event | category | flops | bytes accessed | tf_op | source)
XLA Modules:
  0.0 254.6 jit_solution(13685909091110876890)
XLA Ops:
  0.0 251.2 %fused.1 = f32[256,64,128]{2,1,0:T(8,128)S(1)} custom-call(f32[32,512,128]{2,1,0:T(8,128)} %bitcast.10, f32[256,256]{1,0:T(8,128)} %mix_ref.1, f32[256,256]{1,0:T(8,128)} %w_in_ref.1, f32[256,256]{1,0:T(8,128)} %w_out_ref.1, f32[32,256]{1,0:T(8,128)} %bitcast.11, f32[32,256]{1,0:T(8,128)} %bitcast.12, f32[32,256]{1,0:T(8,128)} %bitcast.13, ...), custom_call_target="tpu_custom_call" | custom-call | tf_op jit(solution)/shard_map/fused/pallas_call | solution.py:866
  251.2 3.4 %copy.13 = f32[256,16,4,128]{3,2,1,0:T(4,128)} copy(f32[256,16,4,128]{3,2,1,0:T(4,128)S(1)} %bitcast.9) | data formatting | bytes 16777216

commit v2 on v1

--- a/solution.py
+++ b/solution.py
@@ -284,7 +284,7 @@
 
 MESH = pl.DeviceIdType.MESH
 LANES = 128
-AHEAD = 3
+AHEAD = 4
 
 
 def cosine(index, length):
@@ -355,7 +355,8 @@
     lane_y, lane_n = log2(y_local), log2(ny)
 
     me_sub = lax.axis_index("sub")
-    me_wide = lax.axis_index("sp") * n_rep + lax.axis_index("rep")
+    me_sp, me_rep = lax.axis_index("sp"), lax.axis_index("rep")
+    me_wide = me_sp * n_rep + me_rep
     me = me_wide * n_sub + me_sub
 
     def place(w, s):
@@ -363,6 +364,18 @@
 
     def place_flat(index):
         return place(index // n_sub, index % n_sub)
+
+    def wide_peer(k):
+        return (me_sp + k // n_rep) % n_sp * n_rep + (me_rep + k % n_rep) % n_rep
+
+    def flat_peer(k):
+        w = (me_sp + k // (n_rep * n_sub)) % n_sp * n_rep + (me_rep + k % n_rep) % n_rep
+        return w, (me_sub + k // n_rep % n_sub) % n_sub
+
+    def turn(i, n):
+        near = n // n_sp
+        late = i // (n - near)
+        return (1 - late) * (near + i) + late * (n - 1 - i)
 
     def loop(n, body):
         def step(i, carry):
@@ -428,7 +441,7 @@
     lane = iota((1, LANES), 1)
 
     def e_copy(xc, k):
-        w = (me_wide + k) % wide
+        w = wide_peer(k)
         xs = pl.ds(xc * xc_size, xc_size)
         return pltpu.make_async_remote_copy(
             src_ref=se.at[w, :, xs],
@@ -443,7 +456,7 @@
     hc_size = x_local // hchunks
 
     def h_copy(hc, k):
-        w = (me_wide + k) % wide
+        w = wide_peer(k)
         xs = pl.ds(hc * hc_size, hc_size)
         return pltpu.make_async_remote_copy(
             src_ref=sh.at[w, xs],
@@ -455,19 +468,20 @@
         )
 
     def peers(make, what, n=wide):
-        def step(k, carry):
-            getattr(make(k), what)()
+        def step(i, carry):
+            getattr(make(turn(i, n)), what)()
             return carry
 
-        lax.fori_loop(1, n, step, 0)
+        lax.fori_loop(0, n - 1, step, 0)
 
     zero = jnp.zeros((own, LANES), jnp.float32)
 
     def transform(xc, squares):
         fetch(xc).wait()
 
-        def one(d, carry):
+        def one(i, carry):
             left, sq = carry
+            d = wide_peer(turn(i, wide))
             groups = []
             for xi in range(xc_size):
                 row = (xc * xc_size + xi) * ny + d * y_local
@@ -483,19 +497,20 @@
                 sq = sq + jnp.sum(part * part, axis=0)
             more = pltpu.roll(res[:, LANES : 2 * LANES], d * y_local, axis=1)
             left = jnp.where((lane >> lane_y) == d, more, left)
+
+            @pl.when(jnp.logical_and(xc == 0, i == 1))
+            def _():
+                pl.semaphore_wait(barrier, count - 1)
+
+            @pl.when(i >= 1)
+            def _():
+                e_copy(xc, turn(i - 1, wide)).start()
+
             return left, sq
 
         left = jnp.zeros((xc_size * own, LANES), jnp.float32)
         left, squares = lax.fori_loop(0, wide, one, (left, squares))
         lf[pl.ds(xc * xc_size, xc_size)] = left.reshape(xc_size, own, LANES)
-
-        @pl.when(xc == 1)
-        def _():
-            pl.semaphore_wait(barrier, count - 1)
-
-        @pl.when(xc >= 1)
-        def _():
-            peers(lambda k: e_copy(xc - 1, k), "start")
 
         return squares
 
@@ -547,16 +562,13 @@
         part = jnp.where(rest, c >> log2(LANES // 2), part)
         return k, part, c & (ny - 1)
 
-    def y_entry(pt, mt, p, m, power):
+    def y_entry(pt, mt, p, m, forward):
         kp, s, y = p_meta(pt, p)
         km, part, b = m_meta(mt, m)
         value = cosine((y * b + (ny // 4) * (s + part)) & (ny - 1), ny)
-        norm = jnp.where(km == 0, math.sqrt(1.0 / nz), math.sqrt(2.0 / nz))
-        scale = norm if power else 1.0 / norm
-        if not power:
+        scale = jnp.where(km == 0, math.sqrt(nz), math.sqrt(nz / 2.0))
+        if forward:
             scale = scale * (1.0 / nz)
-        else:
-            scale = 1.0 / scale
         return jnp.where(kp == km, value * scale, 0.0)
 
     square = (LANES, LANES)
@@ -567,8 +579,8 @@
         for t in range(mtiles):
             cut = slice(t * LANES, (t + 1) * LANES)
             a, b = iota(square, 0), iota(square, 1)
-            yf_hi[rows, cut], yf_lo[rows, cut] = split(y_entry(i, t, a, b, False))
-            yi_hi[rows, cut], yi_lo[rows, cut] = split(y_entry(t, i, b, a, True))
+            yf_hi[rows, cut], yf_lo[rows, cut] = split(y_entry(i, t, a, b, True))
+            yi_hi[rows, cut], yi_lo[rows, cut] = split(y_entry(t, i, b, a, False))
 
     def build_x(i):
         shape = (LANES, nx * 8)
@@ -581,7 +593,6 @@
         rows = pl.ds(pl.multiple_of(i * LANES, LANES), LANES)
         xt_hi[rows], xt_lo[rows] = split(value)
 
-    peers(lambda k: e_copy(xchunks - 1, k), "start")
     for copy in x_copies:
         copy.start()
     for copy in own_copies:
@@ -688,15 +699,15 @@
         start = tuple(jnp.zeros((chain, LANES), jnp.float32) for _ in range(wide))
         done = lax.fori_loop(0, x_local, one, start)
         for d in range(wide):
-            ls[s, d] = done[d]
+            other = pltpu.roll(done[d][chain // 2 :], LANES // 2, axis=1)
+            ls[s, d] = jnp.where(lane < LANES // 2, done[d][: chain // 2], other)
 
     loop(n_sub, gather_rest)
 
     b_rows = pl.ds(pl.multiple_of(first, 8), chain)
 
     def b_copy(k):
-        index = (me + k) % count
-        w, s = index // n_sub, index % n_sub
+        w, s = flat_peer(k)
         return pltpu.make_async_remote_copy(
             src_ref=bs.at[w, pl.ds(s * x_local, x_local)],
             dst_ref=rb.at[:, b_rows],
@@ -707,11 +718,10 @@
         )
 
     def l_copy(k):
-        index = (me + k) % count
-        w, s = index // n_sub, index % n_sub
+        w, s = flat_peer(k)
         return pltpu.make_async_remote_copy(
             src_ref=ls.at[s, w],
-            dst_ref=rl.at[b_rows],
+            dst_ref=rl.at[me],
             send_sem=l_send.at[k],
             recv_sem=l_recv.at[k],
             device_id=place(w, s),
@@ -720,7 +730,7 @@
 
     peers(b_copy, "start", count)
     own_b = pltpu.make_async_copy(bs.at[me_wide, pl.ds(me_sub * x_local, x_local)], rb.at[:, b_rows], b_send.at[0])
-    own_l = pltpu.make_async_copy(ls.at[me_sub, me_wide], rl.at[b_rows], l_send.at[0])
+    own_l = pltpu.make_async_copy(ls.at[me_sub, me_wide], rl.at[me], l_send.at[0])
     own_b.start()
     own_l.start()
     peers(l_copy, "start", count)
@@ -737,7 +747,10 @@
     peers(l_copy, "wait", count)
     loop(xchunks, lambda xc: peers(lambda k: e_copy(xc, k), "wait"))
     mix = split(mats[0])
-    rest = dot3(mix, split(rl[...]))
+    packed = rl[...].reshape(chans // 2, LANES)
+    other = pltpu.roll(packed, LANES // 2, axis=1).reshape(rl.shape)
+    rest = jnp.concatenate([rl[...], other], axis=1).reshape(chans, LANES)
+    rest = dot3(mix, split(rest))
     lows = lane < y_local
     blank = jnp.zeros((chans, LANES), jnp.float32)
 
@@ -778,7 +791,7 @@
             dst_ref=held.at[k],
             send_sem=t_send.at[k],
             recv_sem=t_recv.at[k],
-            device_id=place_flat((me + k) % count),
+            device_id=place(*flat_peer(k)),
             device_id_type=MESH,
         )
 
@@ -840,7 +853,7 @@
     mtiles = 2 * ltile + 1
     parts = nz * y_local // LANES // 2
     size = nz * y_local
-    xchunks, hchunks = 4, x_local * y_local // 8
+    xchunks, hchunks = 4, x_local // 1
     f32, bf = jnp.float32, jnp.bfloat16
     vmem = lambda *shape: pltpu.VMEM(shape, f32)
     table = lambda *shape: pltpu.VMEM(shape, bf)
@@ -855,8 +868,8 @@
         vmem(wide, parts, x_local, own, LANES), vmem(wide, x_local, parts, own, LANES), vmem(x_local, own, LANES),
         vmem(parts, x_local, chans, LANES), vmem(x_local, parts, chans, LANES),
         vmem(tiles, nx, chain, LANES), vmem(sub8, mtiles, nx * 8, LANES),
-        vmem(wide, nx, chain, LANES), vmem(nx, chain, LANES), vmem(n_sub, wide, chain, LANES),
-        vmem(x_local, chans, LANES), vmem(chans, LANES), vmem(count, 8, LANES), vmem(6, chans, LANES),
+        vmem(wide, nx, chain, LANES), vmem(nx, chain, LANES), vmem(n_sub, wide, chain // 2, LANES),
+        vmem(x_local, chans, LANES), vmem(count, chain // 2, LANES), vmem(count, 8, LANES), vmem(6, chans, LANES),
         dma(xchunks), dma(10), dma(tiles + 2), dma(xchunks, wide), dma(xchunks, wide), dma(hchunks, wide),
         dma(hchunks, wide), dma(tiles, n_sub), dma(tiles, n_sub), dma(count), dma(count), dma(count), dma(count),
         dma(count), dma(count),
@@ -895,11 +908,11 @@
         kz * y_local == LANES
         and nz == 4 * kz
         and nx == kz == ny
-        and own % (8 * n_sub) == 0
+        and own % (16 * n_sub) == 0
+        and lax.axis_size("sp") > 1
         and own % (own * wide // GROUPS) == 0
-        and x_local * y_local <= LANES
+        and 2 * x_local * y_local <= LANES
         and x_local % 4 == 0
-        and 8 % y_local == 0
         and (kz // 2 * ny) % LANES == 0
     )
 

time: 256 us -> 247 us (0.965)
  Pallas kernels: 251 us -> 243 us
    pallas_call x1, Pallas kernels: 251 us -> 243 us  [fused(): pl.pallas_call(functools.partial(fused_kernel, (n_sp, n_sub, n_rep, kz)),...]
where the time goes in v2:
time: 247 us
  Pallas kernels  243 us (98%)
  local copies, waits for them, and re-layouts  3.4 us (1%)
    pallas_call x1, Pallas kernels, fused(): pl.pallas_call(functools.partial(fused_kernel, (n_sp, n_sub, n_rep, kz)),...  243 us

profile of v2, /device:TPU:0, one launch (start us, length us, event | category | flops | bytes accessed | tf_op | source)
XLA Modules:
  0.0 246.9 jit_solution(13119312019791857160)
XLA Ops:
  0.0 243.5 %fused.1 = f32[256,64,128]{2,1,0:T(8,128)S(1)} custom-call(f32[32,512,128]{2,1,0:T(8,128)} %bitcast.10, f32[256,256]{1,0:T(8,128)} %mix_ref.1, f32[256,256]{1,0:T(8,128)} %w_in_ref.1, f32[256,256]{1,0:T(8,128)} %w_out_ref.1, f32[32,256]{1,0:T(8,128)} %bitcast.11, f32[32,256]{1,0:T(8,128)} %bitcast.12, f32[32,256]{1,0:T(8,128)} %bitcast.13, ...), custom_call_target="tpu_custom_call" | custom-call | tf_op jit(solution)/shard_map/fused/pallas_call | solution.py:879
  243.5 3.4 %copy.13 = f32[256,16,4,128]{3,2,1,0:T(4,128)} copy(f32[256,16,4,128]{3,2,1,0:T(4,128)S(1)} %bitcast.9) | data formatting | bytes 16777216

commit v3 on v2

--- a/solution.py
+++ b/solution.py
@@ -285,6 +285,7 @@
 MESH = pl.DeviceIdType.MESH
 LANES = 128
 AHEAD = 4
+PUMP = 4
 
 
 def cosine(index, length):
@@ -399,15 +400,11 @@
         rows = pl.ds(i * (xc_size * ny), xc_size * ny)
         return pltpu.make_async_copy(field_ref.at[:, rows], fld.at[:, rows], fld_sem.at[i])
 
-    for i in range(xchunks):
-        fetch(i).start()
+    fetch(0).start()
     params = [(mix_ref, mats.at[0]), (w_in_ref, mats.at[1]), (w_out_ref, mats.at[2])]
     params += [(fx_ref, facs.at[0]), (fy_ref, facs.at[1]), (fz_ref, facs.at[2])]
     params += [(gain_ref, vecs.at[0]), (bias_ref, vecs.at[1]), (b_in_ref, vecs.at[2]), (b_out_ref, vecs.at[3])]
     param_copies = [pltpu.make_async_copy(a, b, par_sem.at[i]) for i, (a, b) in enumerate(params)]
-    for copy in param_copies:
-        copy.start()
-
     def coef(j):
         low_k = jnp.where(j == 1, half, j >> 1)
         low_s = jnp.where(j == 1, 0, j & 1)
@@ -434,6 +431,11 @@
         a = iota((stepr, size), 0) + i * stepr
         b = iota((stepr, size), 1)
         g_hi[rows], g_lo[rows] = split(g_entry(a, b))
+
+    def build_back(i):
+        rows = pl.ds(pl.multiple_of(i * stepr, stepr), stepr)
+        a = iota((stepr, size), 0) + i * stepr
+        b = iota((stepr, size), 1)
         gi_hi[rows], gi_lo[rows] = split(g_entry(b, a))
 
     loop(size // stepr, build_g)
@@ -478,6 +480,11 @@
 
     def transform(xc, squares):
         fetch(xc).wait()
+
+        @pl.when(xc + 1 < xchunks)
+        def _():
+            fetch(xc + 1).start()
+
 
         def one(i, carry):
             left, sq = carry
@@ -516,7 +523,7 @@
 
     squares = lax.fori_loop(0, xchunks, transform, zero)
     for copy in param_copies:
-        copy.wait()
+        copy.start()
 
     def x_src(t, s):
         cs = pl.ds(pl.multiple_of(s * chain, 8), chain)
@@ -598,8 +605,11 @@
     for copy in own_copies:
         copy.start()
     loop(tiles, build_y)
+    loop(size // stepr, build_back)
     loop(2 * nx * 8 // LANES, build_x)
 
+    for copy in param_copies:
+        copy.wait()
     fy_t[...] = jnp.transpose(facs[1])
     fz_t[...] = jnp.transpose(facs[2])
     first = me_wide * own + me_sub * chain
@@ -795,7 +805,15 @@
             device_id_type=MESH,
         )
 
+    def arrive(hc):
+        peers(lambda k: h_copy(hc, k), "wait")
+
+        @pl.when(hc + AHEAD < hchunks)
+        def _():
+            peers(lambda k: h_copy(hc + AHEAD, k), "start")
+
     peers(t_copy, "start", count)
+    loop(PUMP, arrive)
     peers(t_copy, "wait", count)
     total = jnp.sum(held[...], axis=0)
     cells_group = per_group * nx * ny * nz
@@ -813,12 +831,7 @@
     cols[5] = jnp.broadcast_to(shift, (chans, LANES))
 
     def late(hc, carry):
-        peers(lambda k: h_copy(hc, k), "wait")
-
-        @pl.when(hc + AHEAD < hchunks)
-        def _():
-            peers(lambda k: h_copy(hc + AHEAD, k), "start")
-
+        pl.when(hc >= PUMP)(functools.partial(arrive, hc))
         w_in, w_out = split(mats[1]), split(mats[2])
         factor, offset = cols[4, :, 0:1], cols[5, :, 0:1]
         b_in, b_out = cols[2, :, 0:1], cols[3, :, 0:1]
@@ -853,7 +866,7 @@
     mtiles = 2 * ltile + 1
     parts = nz * y_local // LANES // 2
     size = nz * y_local
-    xchunks, hchunks = 4, x_local // 1
+    xchunks, hchunks = 4, x_local
     f32, bf = jnp.float32, jnp.bfloat16
     vmem = lambda *shape: pltpu.VMEM(shape, f32)
     table = lambda *shape: pltpu.VMEM(shape, bf)

time: 247 us -> 245 us (level)
  no operation moved by 1% of the time
where the time goes in v3:
time: 245 us; the launch traced here: 244 us
  Pallas kernels  241 us (98%)
  local copies, waits for them, and re-layouts  3.4 us (1%)
    pallas_call x1, Pallas kernels, fused(): pl.pallas_call(functools.partial(fused_kernel, (n_sp, n_sub, n_rep, kz)),...  241 us

profile of v3, /device:TPU:0, one launch (start us, length us, event | category | flops | bytes accessed | tf_op | source)
XLA Modules:
  0.0 244.4 jit_solution(16821005824265101658)
XLA Ops:
  0.0 241.0 %fused.1 = f32[256,64,128]{2,1,0:T(8,128)S(1)} custom-call(f32[32,512,128]{2,1,0:T(8,128)} %bitcast.10, f32[256,256]{1,0:T(8,128)} %mix_ref.1, f32[256,256]{1,0:T(8,128)} %w_in_ref.1, f32[256,256]{1,0:T(8,128)} %w_out_ref.1, f32[32,256]{1,0:T(8,128)} %bitcast.11, f32[32,256]{1,0:T(8,128)} %bitcast.12, f32[32,256]{1,0:T(8,128)} %bitcast.13, ...), custom_call_target="tpu_custom_call" | custom-call | tf_op jit(solution)/shard_map/fused/pallas_call | solution.py:892
  241.0 3.4 %copy.13 = f32[256,16,4,128]{3,2,1,0:T(4,128)} copy(f32[256,16,4,128]{3,2,1,0:T(4,128)S(1)} %bitcast.9) | data formatting | bytes 16777216

commit v4 on v3

--- a/solution.py
+++ b/solution.py
@@ -376,7 +376,8 @@
     def turn(i, n):
         near = n // n_sp
         late = i // (n - near)
-        return (1 - late) * (near + i) + late * (n - 1 - i)
+        far = near + (i + near * (n_sp // 2 - 1)) % (n - near)
+        return (1 - late) * far + late * (n - 1 - i)
 
     def loop(n, body):
         def step(i, carry):
@@ -600,13 +601,13 @@
         rows = pl.ds(pl.multiple_of(i * LANES, LANES), LANES)
         xt_hi[rows], xt_lo[rows] = split(value)
 
+    loop(2 * nx * 8 // LANES, build_x)
     for copy in x_copies:
         copy.start()
     for copy in own_copies:
         copy.start()
     loop(tiles, build_y)
     loop(size // stepr, build_back)
-    loop(2 * nx * 8 // LANES, build_x)
 
     for copy in param_copies:
         copy.wait()

time: 245 us -> 244 us (level)
  no operation moved by 1% of the time
where the time goes in v4:
time: 244 us; the launch traced here: 243 us
  Pallas kernels  240 us (98%)
  local copies, waits for them, and re-layouts  3.4 us (1%)
    pallas_call x1, Pallas kernels, fused(): pl.pallas_call(functools.partial(fused_kernel, (n_sp, n_sub, n_rep, kz)),...  240 us

profile of v4, /device:TPU:0, one launch (start us, length us, event | category | flops | bytes accessed | tf_op | source)
XLA Modules:
  0.0 243.5 jit_solution(11594547127716490110)
XLA Ops:
  0.0 240.1 %fused.1 = f32[256,64,128]{2,1,0:T(8,128)S(1)} custom-call(f32[32,512,128]{2,1,0:T(8,128)} %bitcast.10, f32[256,256]{1,0:T(8,128)} %mix_ref.1, f32[256,256]{1,0:T(8,128)} %w_in_ref.1, f32[256,256]{1,0:T(8,128)} %w_out_ref.1, f32[32,256]{1,0:T(8,128)} %bitcast.11, f32[32,256]{1,0:T(8,128)} %bitcast.12, f32[32,256]{1,0:T(8,128)} %bitcast.13, ...), custom_call_target="tpu_custom_call" | custom-call | tf_op jit(solution)/shard_map/fused/pallas_call | solution.py:893
  240.1 3.4 %copy.13 = f32[256,16,4,128]{3,2,1,0:T(4,128)} copy(f32[256,16,4,128]{3,2,1,0:T(4,128)S(1)} %bitcast.9) | data formatting | bytes 16777216
